TPU v7x, 32 devices: a whole 2x2x4 slice. The times are simulated.
32 devices in a mesh: frame: 32 (over z, y, x, core), segment: 1.
Axes of the slice: x: 2, y: 2, z: 4, core: 2. Of those that a mesh axis runs over, the one named last changes fastest.
Arguments:
- state: bfloat16 [1, 1024, 3072], P('segment', 'frame'), may hold values from -6 to 6
- modulation: float32 [1, 32, 7, 3072], P('segment'), may hold values from -3 to 3
- noise_level: int32 [4], replicated, may hold values from 0 to 31
- frame_mask: int32 [4, 4], replicated, may hold values from 0 to 1, as said below
- offset: int32 [1], replicated, may hold values from 1 to 3
Outputs:
- next_state: bfloat16 [1, 1024, 3072], P('segment', 'frame')
Inputs may be any that keep to these rules, and one draw needn't show every extreme that they name: frame_mask[i, i] is 1 and frame_mask[i, j] is 0 for j > i.
All inputs are finite; a program needn't handle non-finite values.
Results may differ from a plain program's by a relative error of at most 0.017.
Values may be sent and summed in bfloat16 or wider, within the bound.
A program may use at most 128 MiB of HBM per device.

v0:
```python
import math

import jax
import jax.numpy as jnp
from jax import lax
from jax.sharding import PartitionSpec as P

HEAD = 128
FRAME_TOK = 256


epsilon = 1e-06
negative = -1e30


def passed_along(shard, axis, by):
    peers = lax.axis_size(axis)
    return lax.ppermute(shard, axis, [(i, (i + by) % peers) for i in range(peers)])


def normalize(values):
    widened = values.astype(jnp.float32)
    square_mean = jnp.mean(widened * widened, axis=-1, keepdims=True)
    return (widened * lax.rsqrt(square_mean + epsilon)).astype(jnp.bfloat16)


def modulate(normed, modifiers, column):
    scaled = (
        normed.astype(jnp.float32) * (1.0 + modifiers[..., column, :])
        + modifiers[..., column + 1, :]
    )
    return scaled.astype(jnp.bfloat16)


def body(state, modulation, noise_level, frame_mask, offset):
    hidden = state[0]
    level_table = modulation[0]
    tok_rows, model_width = hidden.shape
    head_count = model_width // HEAD
    devices = lax.axis_size("frame")
    position = lax.axis_index("frame")
    frame_span = FRAME_TOK // tok_rows
    span_bits = frame_span.bit_length() - 1
    bit_total = devices.bit_length() - 1
    frame_mods = jnp.take(level_table, noise_level, axis=0)
    own_frame = position // frame_span
    own_mods = lax.dynamic_index_in_dim(frame_mods, own_frame, 0, keepdims=False)
    normed = normalize(hidden)
    queries = modulate(normed, own_mods, 0)
    query_sets = ((queries, own_frame),)
    prepared = []
    rows_given, frame_given = query_sets[0]
    mask_row = lax.dynamic_index_in_dim(frame_mask, frame_given, 0, keepdims=False)
    prepared.append((rows_given.reshape(rows_given.shape[0], head_count, HEAD), mask_row))
    scale_factor = 1.0 / math.sqrt(HEAD)
    block_rows = 512

    def frames_of(first_row, rows_here):
        return (
            first_row + tok_rows * jnp.arange(rows_here // tok_rows, dtype=jnp.int32)
        ) // FRAME_TOK

    def attend(running, key_rows, value_rows, shard_frames):
        rows_here = key_rows.shape[0]
        key_heads = key_rows.reshape(rows_here, head_count, HEAD)
        value_heads = value_rows.reshape(rows_here, head_count, HEAD)
        updated = []
        for (query_heads, mask_row), state_now in zip(prepared, running):
            shard_allowed = jnp.take(mask_row, shard_frames) == 1
            allowed = jnp.broadcast_to(
                shard_allowed[:, None], (shard_frames.shape[0], tok_rows)
            ).reshape(rows_here)

            def update(previous, query_heads=query_heads, allowed=allowed):
                run_max, denominator, accumulated = previous
                scores = (
                    jnp.einsum(
                        "thd,rhd->htr", query_heads, key_heads, preferred_element_type=jnp.float32
                    )
                    * scale_factor
                )
                scores = jnp.where(allowed[None, None, :], scores, negative)
                new_max = jnp.maximum(run_max, jnp.max(scores, axis=-1))
                weights = jnp.where(
                    allowed[None, None, :], jnp.exp(scores - new_max[..., None]), 0.0
                ).astype(jnp.bfloat16)
                factor = jnp.exp(run_max - new_max)
                denominator = denominator * factor + jnp.sum(weights.astype(jnp.float32), axis=-1)
                accumulated = accumulated * factor[..., None] + jnp.einsum(
                    "htr,rhd->htd", weights, value_heads, preferred_element_type=jnp.float32
                )
                return (new_max, denominator, accumulated)

            updated.append(
                lax.cond(jnp.any(shard_allowed), update, lambda previous: previous, state_now)
            )
        return tuple(updated)

    initial = tuple(
        (
            (
                jnp.full((head_count, heads_given.shape[0]), negative, jnp.float32),
                jnp.zeros((head_count, heads_given.shape[0]), jnp.float32),
                jnp.zeros((head_count, heads_given.shape[0], HEAD), jnp.float32),
            )
            for heads_given, _unused in prepared
        )
    )
    own_keys = modulate(normed, own_mods, 2)
    own_values = modulate(normed, own_mods, 4)

    def consume_ready(carried, block_pieces, block_start):
        rows_here = block_pieces[0].shape[0]
        return attend(carried, block_pieces[0], block_pieces[1], frames_of(block_start, rows_here))

    running = initial
    pieces = (
        lax.all_gather(own_keys, "frame", axis=0, tiled=True),
        lax.all_gather(own_values, "frame", axis=0, tiled=True),
    )
    rows_here = pieces[0].shape[0]
    block_count = rows_here // block_rows
    stacked = tuple((member.reshape(block_count, block_rows, member.shape[1]) for member in pieces))
    starts = block_rows * jnp.arange(block_count, dtype=jnp.int32)

    def advance(carried, block_item):
        return (consume_ready(carried, block_item[0], block_item[1]), None)

    running, _unused = lax.scan(advance, running, (stacked, starts))
    results = []
    for run_max, denominator, accumulated in running:
        merged = accumulated / denominator[..., None]
        results.append(
            jnp.transpose(merged, (1, 0, 2))
            .reshape(merged.shape[1], model_width)
            .astype(jnp.bfloat16)
        )
    attention = results[0]
    section_rows = (
        hidden.astype(jnp.float32) + own_mods[6] * attention.astype(jnp.float32)
    ).astype(jnp.bfloat16)
    passed = passed_along(section_rows, "segment", 1)
    distance = (devices - offset[0] * frame_span % devices) % devices
    rolled = passed
    for bit_index in range(span_bits, bit_total):
        shifted = passed_along(rolled, "frame", 1 << bit_index)
        rolled = jnp.where(distance >> bit_index & 1 == 1, shifted, rolled)
    finished = jnp.where(lax.axis_index("segment") == 0, rolled, passed)
    return finished[None]


def solution(mesh):
    return jax.shard_map(
        body,
        mesh=mesh,
        in_specs=(P("segment", "frame", None), P("segment", None, None, None), P(), P(), P()),
        out_specs=P("segment", "frame", None),
        check_vma=False,
    )
```

profile of v0, /device:TPU:25, one launch (start us, length us, event | category | flops | bytes accessed | tf_op | source)
XLA Modules:
  0.0 212.2 jit_solution(671655326583955405)
XLA Ops:
  6.5 0.7 compare_and_fusion
  7.2 0.7 compare_select_fusion.8
  7.9 5.1 %copy.26 = f32[1,32,7,3072]{3,2,1,0:T(8,128)} copy(f32[1,32,7,3072]{3,1,2,0:T(8,128)} %param.10) | data formatting | bytes 5505024 | tf_op args[1]
  13.0 0.6 dynamic-slice
  13.5 2.5 %gather_fusion.1 = f32[4,7,3072]{2,1,0:T(8,128)S(1)} fusion(f32[32,7,3072]{2,1,0:T(8,128)} %bitcast.81, s32[1024]{0:T(1024)S(1)} %pad_clamp_fusion.1), kind=kCustom, calls=%fused_computation.1 | custom fusion | bytes 688144 | tf_op jit(solution)/shard_map/jit(_take)/gather | solution.py:45
  16.0 0.7 dynamic-slice_select_fusion
  16.7 0.1 fusion.17
  16.8 0.2 fusion.13
  16.9 0.9 fusion.12
  17.9 0.0 all-gather.5.cloned.1.call-start
  17.9 0.7 all-gather.5.cloned.1.call-update
  18.6 0.1 copy.18
  18.8 0.2 add_convert_fusion
  19.0 68.1 %all-gather.3.cloned.1.call-done = bf16[1024,3072]{1,0:T(8,128)(2,1)} async-done(((bf16[32,3072]{1,0:T(8,128)(2,1)}), bf16[1024,3072]{1,0:T(8,128)(2,1)}) %all-gather.3.cloned.1.call-update) | async-done | bytes 6291472 | tf_op jit(solution)/shard_map/all_gather | solution.py:118
  87.1 8.7 %copy.12 = bf16[2,512,3072]{1,2,0:T(8,128)(2,1)} copy(bf16[2,512,3072]{2,1,0:T(8,128)(2,1)} %bitcast.79) | data formatting | bytes 12582912 | tf_op jit(solution)/shard_map/while | solution.py:129
  95.7 61.9 %all-gather.5.cloned.1.call-done = bf16[1024,3072]{1,0:T(8,128)(2,1)} async-done(((bf16[32,3072]{1,0:T(8,128)(2,1)}), bf16[1024,3072]{1,0:T(8,128)(2,1)}) %all-gather.5.cloned.1.call-update) | async-done | bytes 6291472 | tf_op jit(solution)/shard_map/all_gather | solution.py:119
  157.7 8.6 %copy.13 = bf16[2,512,3072]{1,2,0:T(8,128)(2,1)} copy(bf16[2,512,3072]{2,1,0:T(8,128)(2,1)} %bitcast.80) | data formatting | bytes 12582912 | tf_op jit(solution)/shard_map/while | solution.py:129
  166.4 20.7 %while.16 = (s32[]{:T(128)}, f32[24,32]{1,0:T(8,128)S(1)}, f32[24,32]{1,0:T(8,128)S(1)}, f32[24,32,128]{2,1,0:T(8,128)S(1)}, s32[2]{0:T(128)S(1)}, /*index=5*/s3...) while((s32[]{:T(128)}, f32[24,32]{1,0:T(8,128)S(1)}, ...), condition=%wide.region_7.8_spmd, body=%wide.region_1.0_spmd.sunk | while | flops 205852272 | bytes 24633340 | solution.py:129
  166.4 0.6 dynamic_slice.42
  167.0 0.7 fusion.22
  167.7 0.7 gather_fusion
  168.3 0.7 compare_select_fusion.10
  169.0 1.3 compare_reduce_fusion.2
  170.8 5.9 %conditional.2 = ((f32[24,32]{1,0:T(8,128)S(1)}, f32[24,32]{1,0:T(8,128)S(1)}, f32[24,32,128]{2,1,0:T(8,128)S(1)})) conditional(s32[]{:T(128)} %convert_element_type.143, (f32[24,32]{1,0:T(8,128)S(1)}, f32[24,32]{1,0:T(8,128)S(1)}, f32[24,32,128]{2,1,0:T(8,128)S(1)}) %tuple.52, (s32[16,1]{0,1:T(1,128)S(1)}, s32[16,1]{0,1:T(1,128)S(1)}, ...), branch_computations={%region_3.3_spmd, %region_4.6_spmd} | conditional | flops 205850192 | bytes 24628484 | solution.py:95
  170.9 0.1 broadcast_in_dim.66
  170.9 0.1 broadcast_in_dim.67
  171.0 3.3 %constant_dynamic-slice_fusion = (bf16[1,512,3072]{1,2,0:T(8,128)(2,1)S(1)}, bf16[1,512,3072]{1,2,0:T(8,128)(2,1)S(1)}) fusion(bf16[2,512,3072]{1,2,0:T(8,128)(2,1)} %get-tuple-element.231, s32[]{:T(128)} %get-tuple-element.227, bf16[2,512,3072]{1,2,0:T(8,128)(2,1)} %get-tuple-element.226), kind=kLoop, calls=%fused_computation.14 | loop fusion | bytes 12582916 | tf_op jit(solution)/shard_map/while/body/jit(dynamic_index_in_dim)/dynamic_slice | solution.py:129
  174.3 0.7 bitcast_reduce_fusion
  175.0 0.5 convert_reduce_fusion
  175.5 1.2 convolution_add_fusion
  176.7 0.6 dynamic_slice.42
  177.3 0.7 fusion.22
  178.0 0.7 gather_fusion
  178.7 0.7 compare_select_fusion.10
  179.3 1.3 compare_reduce_fusion.2
  181.2 5.9 %conditional.2 = ((f32[24,32]{1,0:T(8,128)S(1)}, f32[24,32]{1,0:T(8,128)S(1)}, f32[24,32,128]{2,1,0:T(8,128)S(1)})) conditional(s32[]{:T(128)} %convert_element_type.143, (f32[24,32]{1,0:T(8,128)S(1)}, f32[24,32]{1,0:T(8,128)S(1)}, f32[24,32,128]{2,1,0:T(8,128)S(1)}) %tuple.52, (s32[16,1]{0,1:T(1,128)S(1)}, s32[16,1]{0,1:T(1,128)S(1)}, ...), branch_computations={%region_3.3_spmd, %region_4.6_spmd} | conditional | flops 205850192 | bytes 24628484 | solution.py:95
  181.2 0.1 broadcast_in_dim.66
  181.3 0.1 broadcast_in_dim.67
  181.3 3.3 %constant_dynamic-slice_fusion = (bf16[1,512,3072]{1,2,0:T(8,128)(2,1)S(1)}, bf16[1,512,3072]{1,2,0:T(8,128)(2,1)S(1)}) fusion(bf16[2,512,3072]{1,2,0:T(8,128)(2,1)} %get-tuple-element.231, s32[]{:T(128)} %get-tuple-element.227, bf16[2,512,3072]{1,2,0:T(8,128)(2,1)} %get-tuple-element.226), kind=kLoop, calls=%fused_computation.14 | loop fusion | bytes 12582916 | tf_op jit(solution)/shard_map/while/body/jit(dynamic_index_in_dim)/dynamic_slice | solution.py:129
  184.6 0.7 bitcast_reduce_fusion
  185.3 0.5 convert_reduce_fusion
  185.8 1.2 convolution_add_fusion
  187.1 0.2 fusion.15
  187.3 0.1 collective-permute-start.1
  188.0 5.5 %collective-permute-done.1 = bf16[32,3072]{1,0:T(8,128)(2,1)S(1)} collective-permute-done((bf16[32,3072]{1,0:T(8,128)(2,1)S(1)}, bf16[32,3072]{1,0:T(8,128)(2,1)S(1)}, u32[]{:S(2)}, u32[]{:S(2)}) %collective-permute-start.1) | collective-permute-done | bytes 196640 | tf_op jit(solution)/shard_map/ppermute | solution.py:18
  193.6 0.2 collective-permute-start.2
  193.8 10.9 %collective-permute-done.2 = bf16[32,3072]{1,0:T(8,128)(2,1)S(1)} collective-permute-done((bf16[32,3072]{1,0:T(8,128)(2,1)S(1)}, bf16[32,3072]{1,0:T(8,128)(2,1)S(1)}, u32[]{:S(2)}, u32[]{:S(2)}) %collective-permute-start.2) | collective-permute-done | bytes 196640 | tf_op jit(solution)/shard_map/ppermute | solution.py:18
  204.7 0.7 select_bitcast_fusion
  (29 shorter events, 0.2 us)
Async XLA Ops:
  6.5 12.2 %copy-start = (s32[4,4]{1,0:T(4,128)S(1)}, s32[4,4]{1,0:T(4,128)}, u32[]{:S(2)}) copy-start(s32[4,4]{1,0:T(4,128)} %param.12) | copy-start | bytes 196
  6.5 80.6 %all-gather.3.cloned.1.call-start = ((), (), s32[]{:S(2)}) async-start(), calls=%async_computation | async-start | bytes 6488064 | tf_op jit(solution)/shard_map/all_gather | solution.py:118
  7.9 8.9 %copy-start.1 = (bf16[1,32,3072]{2,1,0:T(8,128)(2,1)S(1)}, bf16[1,32,3072]{2,1,0:T(8,128)(2,1)}, u32[]{:S(2)}) copy-start(bf16[1,32,3072]{2,1,0:T(8,128)(2,1)} %param.9) | copy-start | bytes 589828
  17.9 139.8 %all-gather.5.cloned.1.call-start = ((), (), s32[]{:S(2)}) async-start(), calls=%async_computation.1 | async-start | bytes 6488064 | tf_op jit(solution)/shard_map/all_gather | solution.py:119
  187.3 6.3 %collective-permute-start.1 = (bf16[32,3072]{1,0:T(8,128)(2,1)S(1)}, bf16[32,3072]{1,0:T(8,128)(2,1)S(1)}, u32[]{:S(2)}, u32[]{:S(2)}) collective-permute-start(bf16[32,3072]{1,0:T(8,128)(2,1)S(1)} %collective-permute-done), channel_id=1, source_target_pairs={{0,8},{1,9},{2,10},{3,11},{4,12},{5,13},{6,14},{7,15},{8,16},{9,17... | collective-permute-start | bytes 589832 | tf_op jit(solution)/shard_map/ppermute | solution.py:18
  193.6 11.1 %collective-permute-start.2 = (bf16[32,3072]{1,0:T(8,128)(2,1)S(1)}, bf16[32,3072]{1,0:T(8,128)(2,1)S(1)}, u32[]{:S(2)}, u32[]{:S(2)}) collective-permute-start(bf16[32,3072]{1,0:T(8,128)(2,1)S(1)} %broadcast_select_fusion), channel_id=1, source_target_pairs={{0,16},{1,17},{2,18},{3,19},{4,20},{5,21},{6,22},{7,23},{8,24},{9,... | collective-permute-start | bytes 589832 | tf_op jit(solution)/shard_map/ppermute | solution.py:18
  (1 other events, 0.0 us)
Sparse Core Ops, SparseCore 0:
  18.0 69.0 all-gather.2
  90.0 67.6 all-gather.4
where the time goes:
time: 216 us; the launch traced here: 212 us
  waiting for transfers between devices  147 us (68%)
  local copies, waits for them, and re-layouts  34.9 us (16%)
  between operations  14.2 us (7%)
  other arithmetic  10.4 us (5%)
  matrix products  3.84 us (2%)
    all_gather x1, waiting for transfers between devices, body(): lax.all_gather(own_keys, 'frame', axis=0, tiled=True)  68.1 us
    all_gather x1, waiting for transfers between devices, body(): lax.all_gather(own_values, 'frame', axis=0, tiled=True)  61.9 us
    while x2, local copies, waits for them, and re-layouts, body(): running, _unused = lax.scan(advance, running, (stacked, starts))  17.3 us
    ppermute x3, waiting for transfers between devices, passed_along(): lax.ppermute(shard, axis, [(i, (i + by) % peers) for i in range(peers)])  16.4 us
    dynamic_slice x4, local copies, waits for them, and re-layouts, body(): running, _unused = lax.scan(advance, running, (stacked, starts))  7.68 us
    unnamed x6, local copies, waits for them, and re-layouts  5.16 us
  transfers between devices with their start and end apart: 5, of which 4 were waited for; matrix products, arithmetic and copies ran while one was open for 4% of the time, Pallas kernels for 0%

commit v1 on v0

v1 whole, which is shorter than its diff:
```python
import functools
import math

import jax
import jax.numpy as jnp
from jax import lax
from jax.experimental import pallas as pl
from jax.experimental.pallas import tpu as pltpu
from jax.sharding import PartitionSpec as P

HEAD = 128
FRAME_TOK = 256

epsilon = 1e-06
negative = -1e30


def kernel(
    devices,
    segments,
    heads,
    frames,
    rows,
    level_ref,
    mask_ref,
    offset_ref,
    state_ref,
    mod_ref,
    out_ref,
    local,
    gathered,
    scale_out,
    scales,
    mods,
    normed,
    keys,
    values,
    outgoing,
    local_sem,
    mod_sem,
    state_send,
    state_recv,
    scale_send,
    scale_recv,
    out_send,
    out_recv,
):
    me = lax.axis_index("frame")
    segment = lax.axis_index("segment")
    span = FRAME_TOK // rows
    width = heads * HEAD
    my_head = lax.div(me * heads + devices - 1, devices)
    owner = lax.div(my_head * devices, heads) == me
    my_columns = pl.multiple_of(my_head * HEAD, HEAD)
    my_frame = lax.div(me, span)
    my_row = pl.multiple_of(lax.rem(me, span) * rows, rows)

    fetch = pltpu.make_async_copy(state_ref.at[0], local, local_sem)
    fetch.start()

    def state_copy(head):
        target = lax.div(head * devices, heads)
        columns = pl.ds(pl.multiple_of(head * HEAD, HEAD), HEAD)
        return target, pltpu.make_async_remote_copy(
            src_ref=state_ref.at[0, :, columns],
            dst_ref=gathered.at[my_frame, pl.ds(my_row, rows), :],
            send_sem=state_send.at[head],
            recv_sem=state_recv.at[my_frame],
            device_id={"frame": target},
            device_id_type=pl.DeviceIdType.MESH,
        )

    def scale_copy(head):
        target = lax.div(head * devices, heads)
        return target, pltpu.make_async_remote_copy(
            src_ref=scale_out,
            dst_ref=scales.at[me],
            send_sem=scale_send.at[head],
            recv_sem=scale_recv,
            device_id={"frame": target},
            device_id_type=pl.DeviceIdType.MESH,
        )

    first_head = lax.div(me * heads, devices)

    def for_heads(make, act):
        def step(index, carry):
            head = lax.rem(first_head + index, heads)
            target, copy = make(head)

            @pl.when(target != me)
            def _():
                act(copy)

            return carry

        lax.fori_loop(0, heads, step, 0)

    for_heads(state_copy, lambda copy: copy.start())

    @pl.when(owner)
    def _():
        pltpu.make_async_copy(
            mod_ref.at[0, :, :, pl.ds(my_columns, HEAD)], mods, mod_sem
        ).start()
        pltpu.make_async_copy(
            state_ref.at[0, :, pl.ds(my_columns, HEAD)],
            gathered.at[my_frame, pl.ds(my_row, rows), :],
            state_recv.at[my_frame],
        ).start()

    fetch.wait()
    widened = local[...].astype(jnp.float32)
    square_mean = jnp.sum(widened * widened, axis=-1, keepdims=True) * (1.0 / width)
    factor = lax.rsqrt(square_mean + epsilon)
    diagonal = lax.broadcasted_iota(jnp.int32, (rows, HEAD), 0) == lax.broadcasted_iota(
        jnp.int32, (rows, HEAD), 1
    )
    scale_out[...] = jnp.sum(
        jnp.where(diagonal, factor, 0.0), axis=0, keepdims=True
    )
    for_heads(scale_copy, lambda copy: copy.start())

    nxt = lax.rem(segment + 1, segments)

    def out_copy(place, part):
        target = place * span + part
        return target, pltpu.make_async_remote_copy(
            src_ref=outgoing.at[place, pl.ds(pl.multiple_of(part * rows, rows), rows), :],
            dst_ref=out_ref.at[0, :, pl.ds(my_columns, HEAD)],
            send_sem=out_send.at[target],
            recv_sem=out_recv,
            device_id={"frame": target, "segment": nxt},
            device_id_type=pl.DeviceIdType.MESH,
        )

    def send_place(place, begin):
        def step(part, carry):
            target, copy = out_copy(place, part)
            remote = jnp.logical_or(target != me, nxt != segment)

            @pl.when(remote)
            def _():
                if begin:
                    copy.start()
                else:
                    copy.wait_send()

            if begin:
                @pl.when(jnp.logical_not(remote))
                def _():
                    pltpu.make_async_copy(
                        outgoing.at[place, pl.ds(pl.multiple_of(part * rows, rows), rows), :],
                        out_ref.at[0, :, pl.ds(my_columns, HEAD)],
                        out_recv,
                    ).start()

            return carry

        lax.fori_loop(0, span, step, 0)

    @pl.when(owner)
    def _():
        pltpu.make_async_copy(scale_out, scales.at[me], scale_recv).start()
        values[:, HEAD:] = jnp.ones((frames * FRAME_TOK, HEAD), jnp.bfloat16)
        pltpu.make_async_copy(
            mod_ref.at[0, :, :, pl.ds(my_columns, HEAD)], mods, mod_sem
        ).wait()
        pltpu.make_async_copy(scales, scales, scale_recv).wait()
        for frame in range(frames):
            pltpu.make_async_copy(
                gathered.at[frame], gathered.at[frame], state_recv.at[frame]
            ).wait()
            row_mods = mods[level_ref[frame]]
            for part in range(span):
                column = jnp.sum(
                    jnp.where(diagonal, scales[frame * span + part], 0.0),
                    axis=1,
                    keepdims=True,
                )
                inner = slice(part * rows, (part + 1) * rows)
                outer = slice(frame * FRAME_TOK + part * rows, frame * FRAME_TOK + (part + 1) * rows)
                scaled = (
                    gathered[frame, inner, :].astype(jnp.float32) * column
                ).astype(jnp.bfloat16)
                normed[frame, inner, :] = scaled
                wide = scaled.astype(jnp.float32)
                keys[outer, :] = (
                    wide * (1.0 + row_mods[2:3]) + row_mods[3:4]
                ).astype(jnp.bfloat16)
                values[outer, :HEAD] = (
                    wide * (1.0 + row_mods[4:5]) + row_mods[5:6]
                ).astype(jnp.bfloat16)

        shift = jnp.where(segment == segments - 1, offset_ref[0], 0)
        for place in range(frames):
            frame = lax.rem(place + shift, frames)
            row_mods = mods[level_ref[frame]]
            queries = (
                normed[frame].astype(jnp.float32) * (1.0 + row_mods[0:1]) + row_mods[1:2]
            ).astype(jnp.bfloat16)
            bias = jnp.concatenate(
                [
                    jnp.full(
                        (1, FRAME_TOK),
                        jnp.where(mask_ref[frame, other] == 1, 0.0, negative),
                        jnp.float32,
                    )
                    for other in range(frames)
                ],
                axis=1,
            )
            scores = lax.dot_general(
                queries,
                keys[...],
                (((1,), (1,)), ((), ())),
                preferred_element_type=jnp.float32,
            )
            scores = scores * (1.0 / math.sqrt(HEAD)) + bias
            weights = jnp.exp(scores - jnp.max(scores, axis=-1, keepdims=True)).astype(
                jnp.bfloat16
            )
            summed = jnp.dot(weights, values[...], preferred_element_type=jnp.float32)
            attention = (summed[:, :HEAD] / summed[:, HEAD:]).astype(jnp.bfloat16)
            outgoing[place] = (
                gathered[frame].astype(jnp.float32)
                + row_mods[6:7] * attention.astype(jnp.float32)
            ).astype(jnp.bfloat16)
            send_place(place, True)

    for_heads(state_copy, lambda copy: copy.wait_send())
    for_heads(scale_copy, lambda copy: copy.wait_send())

    @pl.when(owner)
    def _():
        for place in range(frames):
            send_place(place, False)

    pltpu.make_async_copy(out_ref, out_ref, out_recv).wait()


def body(state, modulation, noise_level, frame_mask, offset):
    _, rows, width = state.shape
    _, levels, kinds, _ = modulation.shape
    devices = lax.axis_size("frame")
    segments = lax.axis_size("segment")
    heads = width // HEAD
    frames = devices * rows // FRAME_TOK
    tokens = devices * rows
    smem = pl.BlockSpec(memory_space=pltpu.SMEM)
    hbm = pl.BlockSpec(memory_space=pl.ANY)
    return pl.pallas_call(
        functools.partial(kernel, devices, segments, heads, frames, rows),
        out_shape=jax.ShapeDtypeStruct(state.shape, jnp.bfloat16),
        in_specs=[smem, smem, smem, hbm, hbm],
        out_specs=pl.BlockSpec(memory_space=pltpu.VMEM),
        scratch_shapes=[
            pltpu.VMEM((rows, width), jnp.bfloat16),
            pltpu.VMEM((frames, FRAME_TOK, HEAD), jnp.bfloat16),
            pltpu.VMEM((1, HEAD), jnp.float32),
            pltpu.VMEM((devices, 1, HEAD), jnp.float32),
            pltpu.VMEM((levels, kinds, HEAD), jnp.float32),
            pltpu.VMEM((frames, FRAME_TOK, HEAD), jnp.bfloat16),
            pltpu.VMEM((tokens, HEAD), jnp.bfloat16),
            pltpu.VMEM((tokens, 2 * HEAD), jnp.bfloat16),
            pltpu.VMEM((frames, FRAME_TOK, HEAD), jnp.bfloat16),
            pltpu.SemaphoreType.DMA,
            pltpu.SemaphoreType.DMA,
            pltpu.SemaphoreType.DMA((heads,)),
            pltpu.SemaphoreType.DMA((frames,)),
            pltpu.SemaphoreType.DMA((heads,)),
            pltpu.SemaphoreType.DMA,
            pltpu.SemaphoreType.DMA((devices,)),
            pltpu.SemaphoreType.DMA,
        ],
        compiler_params=pltpu.CompilerParams(has_side_effects=True),
        name="denoise",
    )(noise_level, frame_mask, offset, state, modulation)


def solution(mesh):
    return jax.shard_map(
        body,
        mesh=mesh,
        in_specs=(P("segment", "frame", None), P("segment", None, None, None), P(), P(), P()),
        out_specs=P("segment", "frame", None),
        check_vma=False,
    )
```

time: 216 us -> 34.9 us (0.16); the launches traced: 212 us -> 34.3 us
  waiting for transfers between devices: 147 us -> 0 us
  local copies, waits for them, and re-layouts: 34.9 us -> 6.68 us
  Pallas kernels: 0 us -> 27 us
  between operations: 14.2 us -> 0.66 us
  other arithmetic: 10.4 us -> 0 us
  matrix products: 3.84 us -> 0 us
    all_gather x2 -> x0, waiting for transfers between devices: 130 us -> none  [the longest x1 68.1 us: body(): lax.all_gather(own_keys, 'frame', axis=0, tiled=True)]
    pallas_call x0 -> x1, Pallas kernels: none -> 27 us  [body(): pl.pallas_call(functools.partial(kernel, devices, segments, heads, frames...]
    while x2 -> x0, local copies, waits for them, and re-layouts: 17.3 us -> none  [body(): running, _unused = lax.scan(advance, running, (stacked, starts))]
    ppermute x3 -> x0, waiting for transfers between devices: 16.4 us -> none  [passed_along(): lax.ppermute(shard, axis, [(i, (i + by) % peers) for i in range(peers)])]
    dynamic_slice x5 -> x0, local copies, waits for them, and re-layouts: 8.26 us -> none  [the longest x4 7.68 us: body(): running, _unused = lax.scan(advance, running, (stacked, starts))]
    select_n x7 -> x0, other arithmetic: 3.99 us -> none  [the longest x4 2.65 us: attend(): shard_allowed = jnp.take(mask_row, shard_frames) == 1]
    dot_general x4 -> x0, matrix products: 3.84 us -> none  [the longest x2 2.47 us: update(): jnp.einsum('htr,rhd->htd', weights, value_heads, preferred_element_type=j...]
    gather x3 -> x0, local copies, waits for them, and re-layouts: 3.77 us -> none  [the longest x1 2.46 us: body(): frame_mods = jnp.take(level_table, noise_level, axis=0)]
  transfers between devices with their start and end apart: 5 -> 0, of which waited for: 4 -> 0; matrix products, arithmetic and copies ran while one was open for 4% -> 0% of each run, Pallas kernels for 0% -> 0%
where the time goes in v1:
time: 34.9 us; the launch traced here: 34.3 us
  Pallas kernels  27 us (77%)
  local copies, waits for them, and re-layouts  6.68 us (19%)
  between operations  0.66 us (2%)
    pallas_call x1, Pallas kernels, body(): pl.pallas_call(functools.partial(kernel, devices, segments, heads, frames...  27 us
    unnamed x2, local copies, waits for them, and re-layouts  6.68 us

profile of v1, /device:TPU:25, one launch (start us, length us, event | category | flops | bytes accessed | tf_op | source)
XLA Modules:
  0.0 34.3 jit_solution(2643785131580003897)
XLA Ops:
  0.7 5.1 %copy.6.mod_ref = f32[1,32,7,3072]{3,2,1,0:T(8,128)} copy(f32[1,32,7,3072]{3,1,2,0:T(8,128)} %param.6) | data formatting | bytes 5505024 | tf_op args[1]
  5.7 27.0 %denoise.1 = bf16[1,32,3072]{2,1,0:T(8,128)(2,1)} custom-call(s32[4]{0:T(128)} %level_ref.1, s32[4,4]{1,0:T(4,128)} %mask_ref.1, s32[1]{0:T(128)S(6)} %copy.8.offset_ref, bf16[1,32,3072]{2,1,0:T(8,128)(2,1)} %state_ref.1, f32[1,32,7,3072]{3,2,1,0:T(8,128)} %copy.6.mod_ref), custom_call_target="tpu_custom_call" | custom-call | tf_op jit(solution)/shard_map/denoise/pallas_call | solution.py:252
  32.7 1.6 %copy.9 = bf16[1,32,3072]{2,1,0:T(8,128)(2,1)} copy(bf16[1,32,3072]{2,1,0:T(8,128)(2,1)} %denoise.1) | data formatting | bytes 393216

commit v2 on v1

--- a/solution.py
+++ b/solution.py
@@ -49,65 +49,43 @@
     segment = lax.axis_index("segment")
     span = FRAME_TOK // rows
     width = heads * HEAD
-    my_head = lax.div(me * heads + devices - 1, devices)
-    owner = lax.div(my_head * devices, heads) == me
+    my_head = lax.min(me, heads - 1)
+    owner = me < heads
     my_columns = pl.multiple_of(my_head * HEAD, HEAD)
     my_frame = lax.div(me, span)
     my_row = pl.multiple_of(lax.rem(me, span) * rows, rows)
 
+    nxt = lax.rem(segment + 1, segments)
+    barrier = pltpu.get_barrier_semaphore()
+
+    def greet(peer, peer_segment):
+        pl.semaphore_signal(
+            barrier,
+            inc=1,
+            device_id={"frame": peer, "segment": peer_segment},
+            device_id_type=pl.DeviceIdType.MESH,
+        )
+
+    def greet_reader(index, carry):
+        greet(lax.rem(me + index, devices), segment)
+        return carry
+
+    def greet_writer(head, carry):
+        greet(head, lax.rem(segment + segments - 1, segments))
+        return carry
+
     fetch = pltpu.make_async_copy(state_ref.at[0], local, local_sem)
     fetch.start()
 
-    def state_copy(head):
-        target = lax.div(head * devices, heads)
-        columns = pl.ds(pl.multiple_of(head * HEAD, HEAD), HEAD)
-        return target, pltpu.make_async_remote_copy(
-            src_ref=state_ref.at[0, :, columns],
-            dst_ref=gathered.at[my_frame, pl.ds(my_row, rows), :],
-            send_sem=state_send.at[head],
-            recv_sem=state_recv.at[my_frame],
-            device_id={"frame": target},
-            device_id_type=pl.DeviceIdType.MESH,
-        )
-
-    def scale_copy(head):
-        target = lax.div(head * devices, heads)
-        return target, pltpu.make_async_remote_copy(
-            src_ref=scale_out,
-            dst_ref=scales.at[me],
-            send_sem=scale_send.at[head],
-            recv_sem=scale_recv,
-            device_id={"frame": target},
-            device_id_type=pl.DeviceIdType.MESH,
-        )
-
-    first_head = lax.div(me * heads, devices)
-
-    def for_heads(make, act):
-        def step(index, carry):
-            head = lax.rem(first_head + index, heads)
-            target, copy = make(head)
-
-            @pl.when(target != me)
-            def _():
-                act(copy)
-
-            return carry
-
-        lax.fori_loop(0, heads, step, 0)
-
-    for_heads(state_copy, lambda copy: copy.start())
-
     @pl.when(owner)
     def _():
+        lax.fori_loop(1, devices, greet_reader, 0)
         pltpu.make_async_copy(
             mod_ref.at[0, :, :, pl.ds(my_columns, HEAD)], mods, mod_sem
         ).start()
-        pltpu.make_async_copy(
-            state_ref.at[0, :, pl.ds(my_columns, HEAD)],
-            gathered.at[my_frame, pl.ds(my_row, rows), :],
-            state_recv.at[my_frame],
-        ).start()
+
+    if segments > 1:
+        lax.fori_loop(0, heads, greet_writer, 0)
 
     fetch.wait()
     widened = local[...].astype(jnp.float32)
@@ -119,15 +97,73 @@
     scale_out[...] = jnp.sum(
         jnp.where(diagonal, factor, 0.0), axis=0, keepdims=True
     )
-    for_heads(scale_copy, lambda copy: copy.start())
-
-    nxt = lax.rem(segment + 1, segments)
+
+    greetings = heads - jnp.where(owner, 1, 0)
+    if segments > 1:
+        greetings += jnp.where(owner, devices, 0)
+    pl.semaphore_wait(barrier, greetings)
+
+    def state_copy(head):
+        columns = pl.ds(pl.multiple_of(head * HEAD, HEAD), HEAD)
+        return pltpu.make_async_remote_copy(
+            src_ref=local.at[:, columns],
+            dst_ref=gathered.at[my_frame, pl.ds(my_row, rows), :],
+            send_sem=state_send.at[head],
+            recv_sem=state_recv.at[my_frame],
+            device_id={"frame": head},
+            device_id_type=pl.DeviceIdType.MESH,
+        )
+
+    def scale_copy(head):
+        return pltpu.make_async_remote_copy(
+            src_ref=scale_out,
+            dst_ref=scales.at[me],
+            send_sem=scale_send.at[head],
+            recv_sem=scale_recv.at[my_frame],
+            device_id={"frame": head},
+            device_id_type=pl.DeviceIdType.MESH,
+        )
+
+    def for_heads(act):
+        def step(index, carry):
+            head = lax.rem(me + index, heads)
+
+            @pl.when(head != me)
+            def _():
+                act(head)
+
+            return carry
+
+        lax.fori_loop(0, heads, step, 0)
+
+    def send_rows(head):
+        state_copy(head).start()
+        scale_copy(head).start()
+
+    def end_rows(head):
+        state_copy(head).wait_send()
+        scale_copy(head).wait_send()
+
+    for_heads(send_rows)
+
+    @pl.when(owner)
+    def _():
+        pltpu.make_async_copy(
+            local.at[:, pl.ds(my_columns, HEAD)],
+            gathered.at[my_frame, pl.ds(my_row, rows), :],
+            state_recv.at[my_frame],
+        ).start()
+        pltpu.make_async_copy(scale_out, scales.at[me], scale_recv.at[my_frame]).start()
+
+    def mods_of(frame):
+        level = level_ref[frame]
+        return lambda kind: mods[kind, pl.ds(level, 1), :]
 
     def out_copy(place, part):
         target = place * span + part
         return target, pltpu.make_async_remote_copy(
             src_ref=outgoing.at[place, pl.ds(pl.multiple_of(part * rows, rows), rows), :],
-            dst_ref=out_ref.at[0, :, pl.ds(my_columns, HEAD)],
+            dst_ref=out_ref.at[my_head],
             send_sem=out_send.at[target],
             recv_sem=out_recv,
             device_id={"frame": target, "segment": nxt},
@@ -151,7 +187,7 @@
                 def _():
                     pltpu.make_async_copy(
                         outgoing.at[place, pl.ds(pl.multiple_of(part * rows, rows), rows), :],
-                        out_ref.at[0, :, pl.ds(my_columns, HEAD)],
+                        out_ref.at[my_head],
                         out_recv,
                     ).start()
 
@@ -161,17 +197,17 @@
 
     @pl.when(owner)
     def _():
-        pltpu.make_async_copy(scale_out, scales.at[me], scale_recv).start()
         values[:, HEAD:] = jnp.ones((frames * FRAME_TOK, HEAD), jnp.bfloat16)
         pltpu.make_async_copy(
             mod_ref.at[0, :, :, pl.ds(my_columns, HEAD)], mods, mod_sem
         ).wait()
-        pltpu.make_async_copy(scales, scales, scale_recv).wait()
         for frame in range(frames):
             pltpu.make_async_copy(
                 gathered.at[frame], gathered.at[frame], state_recv.at[frame]
             ).wait()
-            row_mods = mods[level_ref[frame]]
+            arrived = scales.at[pl.ds(frame * span, span)]
+            pltpu.make_async_copy(arrived, arrived, scale_recv.at[frame]).wait()
+            row_mods = mods_of(frame)
             for part in range(span):
                 column = jnp.sum(
                     jnp.where(diagonal, scales[frame * span + part], 0.0),
@@ -186,18 +222,18 @@
                 normed[frame, inner, :] = scaled
                 wide = scaled.astype(jnp.float32)
                 keys[outer, :] = (
-                    wide * (1.0 + row_mods[2:3]) + row_mods[3:4]
+                    wide * (1.0 + row_mods(2)) + row_mods(3)
                 ).astype(jnp.bfloat16)
                 values[outer, :HEAD] = (
-                    wide * (1.0 + row_mods[4:5]) + row_mods[5:6]
+                    wide * (1.0 + row_mods(4)) + row_mods(5)
                 ).astype(jnp.bfloat16)
 
         shift = jnp.where(segment == segments - 1, offset_ref[0], 0)
         for place in range(frames):
             frame = lax.rem(place + shift, frames)
-            row_mods = mods[level_ref[frame]]
+            row_mods = mods_of(frame)
             queries = (
-                normed[frame].astype(jnp.float32) * (1.0 + row_mods[0:1]) + row_mods[1:2]
+                normed[frame].astype(jnp.float32) * (1.0 + row_mods(0)) + row_mods(1)
             ).astype(jnp.bfloat16)
             bias = jnp.concatenate(
                 [
@@ -224,12 +260,11 @@
             attention = (summed[:, :HEAD] / summed[:, HEAD:]).astype(jnp.bfloat16)
             outgoing[place] = (
                 gathered[frame].astype(jnp.float32)
-                + row_mods[6:7] * attention.astype(jnp.float32)
+                + row_mods(6) * attention.astype(jnp.float32)
             ).astype(jnp.bfloat16)
             send_place(place, True)
 
-    for_heads(state_copy, lambda copy: copy.wait_send())
-    for_heads(scale_copy, lambda copy: copy.wait_send())
+    for_heads(end_rows)
 
     @pl.when(owner)
     def _():
@@ -249,9 +284,9 @@
     tokens = devices * rows
     smem = pl.BlockSpec(memory_space=pltpu.SMEM)
     hbm = pl.BlockSpec(memory_space=pl.ANY)
-    return pl.pallas_call(
+    tiles = pl.pallas_call(
         functools.partial(kernel, devices, segments, heads, frames, rows),
-        out_shape=jax.ShapeDtypeStruct(state.shape, jnp.bfloat16),
+        out_shape=pltpu.VMEM((heads, rows, HEAD), jnp.bfloat16),
         in_specs=[smem, smem, smem, hbm, hbm],
         out_specs=pl.BlockSpec(memory_space=pltpu.VMEM),
         scratch_shapes=[
@@ -259,7 +294,7 @@
             pltpu.VMEM((frames, FRAME_TOK, HEAD), jnp.bfloat16),
             pltpu.VMEM((1, HEAD), jnp.float32),
             pltpu.VMEM((devices, 1, HEAD), jnp.float32),
-            pltpu.VMEM((levels, kinds, HEAD), jnp.float32),
+            pltpu.VMEM((kinds, levels, HEAD), jnp.float32),
             pltpu.VMEM((frames, FRAME_TOK, HEAD), jnp.bfloat16),
             pltpu.VMEM((tokens, HEAD), jnp.bfloat16),
             pltpu.VMEM((tokens, 2 * HEAD), jnp.bfloat16),
@@ -269,13 +304,14 @@
             pltpu.SemaphoreType.DMA((heads,)),
             pltpu.SemaphoreType.DMA((frames,)),
             pltpu.SemaphoreType.DMA((heads,)),
-            pltpu.SemaphoreType.DMA,
+            pltpu.SemaphoreType.DMA((frames,)),
             pltpu.SemaphoreType.DMA((devices,)),
             pltpu.SemaphoreType.DMA,
         ],
-        compiler_params=pltpu.CompilerParams(has_side_effects=True),
+        compiler_params=pltpu.CompilerParams(has_side_effects=True, collective_id=0),
         name="denoise",
-    )(noise_level, frame_mask, offset, state, modulation)
+    )(noise_level, frame_mask, offset, state, jnp.swapaxes(modulation, 1, 2))
+    return jnp.swapaxes(tiles, 0, 1).reshape(state.shape)
 
 
 def solution(mesh):

time: 34.9 us -> 25.4 us (0.73); the launches traced: 34.3 us -> 25.2 us
  local copies, waits for them, and re-layouts: 6.68 us -> 0.84 us
  Pallas kernels: 27 us -> 23.7 us
    unnamed x2 -> x0, local copies, waits for them, and re-layouts: 6.68 us -> none
    pallas_call x1, Pallas kernels: 27 us -> 23.7 us  [body(): pl.pallas_call(functools.partial(kernel, devices, segments, heads, frames...]
    reshape x0 -> x1, local copies, waits for them, and re-layouts: none -> 0.76 us  [body(): return jnp.swapaxes(tiles, 0, 1).reshape(state.shape)]
where the time goes in v2:
time: 25.4 us; the launch traced here: 25.2 us
  Pallas kernels  23.7 us (93%)
  local copies, waits for them, and re-layouts  0.84 us (3%)
  between operations  0.67 us (3%)
    pallas_call x1, Pallas kernels, body(): pl.pallas_call(functools.partial(kernel, devices, segments, heads, frames...  23.7 us
    reshape x1, local copies, waits for them, and re-layouts, body(): return jnp.swapaxes(tiles, 0, 1).reshape(state.shape)  0.76 us

profile of v2, /device:TPU:25, one launch (start us, length us, event | category | flops | bytes accessed | tf_op | source)
XLA Modules:
  0.0 25.2 jit_solution(5933890152490581874)
XLA Ops:
  0.7 23.7 %denoise.1 = bf16[24,32,128]{2,1,0:T(8,128)(2,1)S(1)} custom-call(s32[4]{0:T(128)} %level_ref.1, s32[4,4]{1,0:T(4,128)} %mask_ref.1, s32[1]{0:T(128)S(6)} %copy.7.offset_ref, bf16[1,32,3072]{2,1,0:T(8,128)(2,1)} %state_ref.1, f32[1,7,32,3072]{3,2,1,0:T(8,128)} %bitcast.3), custom_call_target="tpu_custom_call" | custom-call | tf_op jit(solution)/shard_map/denoise/pallas_call | solution.py:287
  24.4 0.1 copy.6
  24.5 0.8 %reshape.3 = bf16[1,32,3072]{2,1,0:T(8,128)(2,1)} reshape(bf16[32,24,128]{2,1,0:T(8,128)(2,1)S(1)} %copy.6) | data formatting | bytes 393216 | tf_op jit(solution)/shard_map/reshape | solution.py:314

commit v3 on v2

--- a/solution.py
+++ b/solution.py
@@ -49,8 +49,13 @@
     segment = lax.axis_index("segment")
     span = FRAME_TOK // rows
     width = heads * HEAD
-    my_head = lax.min(me, heads - 1)
-    owner = me < heads
+    def owner_of(head):
+        return lax.div(head * devices, heads)
+
+    my_head = lax.min(lax.div(me * heads + devices - 1, devices), heads - 1)
+    owner = owner_of(my_head) == me
+    group = max(heads * span // devices, 1)
+    group = group if heads % group == 0 else 1
     my_columns = pl.multiple_of(my_head * HEAD, HEAD)
     my_frame = lax.div(me, span)
     my_row = pl.multiple_of(lax.rem(me, span) * rows, rows)
@@ -71,7 +76,7 @@
         return carry
 
     def greet_writer(head, carry):
-        greet(head, lax.rem(segment + segments - 1, segments))
+        greet(owner_of(head), lax.rem(segment + segments - 1, segments))
         return carry
 
     fetch = pltpu.make_async_copy(state_ref.at[0], local, local_sem)
@@ -88,6 +93,59 @@
         lax.fori_loop(0, heads, greet_writer, 0)
 
     fetch.wait()
+    greetings = heads - jnp.where(owner, 1, 0)
+    if segments > 1:
+        greetings += jnp.where(owner, devices, 0)
+    pl.semaphore_wait(barrier, greetings)
+
+    def state_copy(head):
+        columns = pl.ds(pl.multiple_of(head * HEAD, HEAD), HEAD)
+        return pltpu.make_async_remote_copy(
+            src_ref=local.at[:, columns],
+            dst_ref=gathered.at[my_frame, pl.ds(my_row, rows), :],
+            send_sem=state_send.at[head],
+            recv_sem=state_recv.at[my_frame],
+            device_id={"frame": owner_of(head)},
+            device_id_type=pl.DeviceIdType.MESH,
+        )
+
+    def scale_copy(head):
+        return pltpu.make_async_remote_copy(
+            src_ref=scale_out,
+            dst_ref=scales.at[me],
+            send_sem=scale_send.at[head],
+            recv_sem=scale_recv.at[my_frame],
+            device_id={"frame": owner_of(head)},
+            device_id_type=pl.DeviceIdType.MESH,
+        )
+
+    def for_heads(act):
+        def step(index, carry):
+            turned = index - lax.rem(index, group) + lax.rem(index + me, group)
+            head = lax.rem(lax.div(me * heads, devices) + index, heads)
+
+            @pl.when(owner_of(head) != me)
+            def _():
+                act(head)
+
+            return carry
+
+        lax.fori_loop(0, heads, step, 0)
+
+    def end_rows(head):
+        state_copy(head).wait_send()
+        scale_copy(head).wait_send()
+
+    for_heads(lambda head: state_copy(head).start())
+
+    @pl.when(owner)
+    def _():
+        pltpu.make_async_copy(
+            local.at[:, pl.ds(my_columns, HEAD)],
+            gathered.at[my_frame, pl.ds(my_row, rows), :],
+            state_recv.at[my_frame],
+        ).start()
+
     widened = local[...].astype(jnp.float32)
     square_mean = jnp.sum(widened * widened, axis=-1, keepdims=True) * (1.0 / width)
     factor = lax.rsqrt(square_mean + epsilon)
@@ -98,61 +156,10 @@
         jnp.where(diagonal, factor, 0.0), axis=0, keepdims=True
     )
 
-    greetings = heads - jnp.where(owner, 1, 0)
-    if segments > 1:
-        greetings += jnp.where(owner, devices, 0)
-    pl.semaphore_wait(barrier, greetings)
-
-    def state_copy(head):
-        columns = pl.ds(pl.multiple_of(head * HEAD, HEAD), HEAD)
-        return pltpu.make_async_remote_copy(
-            src_ref=local.at[:, columns],
-            dst_ref=gathered.at[my_frame, pl.ds(my_row, rows), :],
-            send_sem=state_send.at[head],
-            recv_sem=state_recv.at[my_frame],
-            device_id={"frame": head},
-            device_id_type=pl.DeviceIdType.MESH,
-        )
-
-    def scale_copy(head):
-        return pltpu.make_async_remote_copy(
-            src_ref=scale_out,
-            dst_ref=scales.at[me],
-            send_sem=scale_send.at[head],
-            recv_sem=scale_recv.at[my_frame],
-            device_id={"frame": head},
-            device_id_type=pl.DeviceIdType.MESH,
-        )
-
-    def for_heads(act):
-        def step(index, carry):
-            head = lax.rem(me + index, heads)
-
-            @pl.when(head != me)
-            def _():
-                act(head)
-
-            return carry
-
-        lax.fori_loop(0, heads, step, 0)
-
-    def send_rows(head):
-        state_copy(head).start()
-        scale_copy(head).start()
-
-    def end_rows(head):
-        state_copy(head).wait_send()
-        scale_copy(head).wait_send()
-
-    for_heads(send_rows)
-
-    @pl.when(owner)
-    def _():
-        pltpu.make_async_copy(
-            local.at[:, pl.ds(my_columns, HEAD)],
-            gathered.at[my_frame, pl.ds(my_row, rows), :],
-            state_recv.at[my_frame],
-        ).start()
+    for_heads(lambda head: scale_copy(head).start())
+
+    @pl.when(owner)
+    def _():
         pltpu.make_async_copy(scale_out, scales.at[me], scale_recv.at[my_frame]).start()
 
     def mods_of(frame):
@@ -229,7 +236,8 @@
                 ).astype(jnp.bfloat16)
 
         shift = jnp.where(segment == segments - 1, offset_ref[0], 0)
-        for place in range(frames):
+        for turn in range(frames):
+            place = jnp.where(2 * me >= devices, turn, (frames - turn) % frames)
             frame = lax.rem(place + shift, frames)
             row_mods = mods_of(frame)
             queries = (

time: 25.4 us -> 23.6 us (0.929)
  the two profiles are of different devices: /device:TPU:25 before, /device:TPU:11 now
where the time goes in v3:
time: 23.6 us; the launch traced here: 23.4 us
  Pallas kernels  21.9 us (93%)
  local copies, waits for them, and re-layouts  0.84 us (4%)
  between operations  0.67 us (3%)
    pallas_call x1, Pallas kernels, body(): pl.pallas_call(functools.partial(kernel, devices, segments, heads, frames...  21.9 us
    reshape x1, local copies, waits for them, and re-layouts, body(): return jnp.swapaxes(tiles, 0, 1).reshape(state.shape)  0.76 us

profile of v3, /device:TPU:11, one launch (start us, length us, event | category | flops | bytes accessed | tf_op | source)
XLA Modules:
  0.0 23.4 jit_solution(3283982210998889472)
XLA Ops:
  0.7 21.9 %denoise.1 = bf16[24,32,128]{2,1,0:T(8,128)(2,1)S(1)} custom-call(s32[4]{0:T(128)} %level_ref.1, s32[4,4]{1,0:T(4,128)} %mask_ref.1, s32[1]{0:T(128)S(6)} %copy.7.offset_ref, bf16[1,32,3072]{2,1,0:T(8,128)(2,1)} %state_ref.1, f32[1,7,32,3072]{3,2,1,0:T(8,128)} %bitcast.3), custom_call_target="tpu_custom_call" | custom-call | tf_op jit(solution)/shard_map/denoise/pallas_call | solution.py:295
  22.6 0.1 copy.6
  22.6 0.8 %reshape.3 = bf16[1,32,3072]{2,1,0:T(8,128)(2,1)} reshape(bf16[32,24,128]{2,1,0:T(8,128)(2,1)S(1)} %copy.6) | data formatting | bytes 393216 | tf_op jit(solution)/shard_map/reshape | solution.py:322

commit v4 on v3

--- a/solution.py
+++ b/solution.py
@@ -49,6 +49,7 @@
     segment = lax.axis_index("segment")
     span = FRAME_TOK // rows
     width = heads * HEAD
+    half = span // math.gcd(span, 2)
     def owner_of(head):
         return lax.div(head * devices, heads)
 
@@ -177,7 +178,7 @@
             device_id_type=pl.DeviceIdType.MESH,
         )
 
-    def send_place(place, begin):
+    def send_place(place, begin, first, last):
         def step(part, carry):
             target, copy = out_copy(place, part)
             remote = jnp.logical_or(target != me, nxt != segment)
@@ -200,7 +201,7 @@
 
             return carry
 
-        lax.fori_loop(0, span, step, 0)
+        lax.fori_loop(first, last, step, 0)
 
     @pl.when(owner)
     def _():
@@ -240,9 +241,6 @@
             place = jnp.where(2 * me >= devices, turn, (frames - turn) % frames)
             frame = lax.rem(place + shift, frames)
             row_mods = mods_of(frame)
-            queries = (
-                normed[frame].astype(jnp.float32) * (1.0 + row_mods(0)) + row_mods(1)
-            ).astype(jnp.bfloat16)
             bias = jnp.concatenate(
                 [
                     jnp.full(
@@ -254,30 +252,35 @@
                 ],
                 axis=1,
             )
-            scores = lax.dot_general(
-                queries,
-                keys[...],
-                (((1,), (1,)), ((), ())),
-                preferred_element_type=jnp.float32,
-            )
-            scores = scores * (1.0 / math.sqrt(HEAD)) + bias
-            weights = jnp.exp(scores - jnp.max(scores, axis=-1, keepdims=True)).astype(
-                jnp.bfloat16
-            )
-            summed = jnp.dot(weights, values[...], preferred_element_type=jnp.float32)
-            attention = (summed[:, :HEAD] / summed[:, HEAD:]).astype(jnp.bfloat16)
-            outgoing[place] = (
-                gathered[frame].astype(jnp.float32)
-                + row_mods(6) * attention.astype(jnp.float32)
-            ).astype(jnp.bfloat16)
-            send_place(place, True)
+            for first in range(0, span, half):
+                inner = slice(first * rows, (first + half) * rows)
+                queries = (
+                    normed[frame, inner, :].astype(jnp.float32) * (1.0 + row_mods(0)) + row_mods(1)
+                ).astype(jnp.bfloat16)
+                scores = lax.dot_general(
+                    queries,
+                    keys[...],
+                    (((1,), (1,)), ((), ())),
+                    preferred_element_type=jnp.float32,
+                )
+                scores = scores * (1.0 / math.sqrt(HEAD)) + bias
+                weights = jnp.exp(scores - jnp.max(scores, axis=-1, keepdims=True)).astype(
+                    jnp.bfloat16
+                )
+                summed = jnp.dot(weights, values[...], preferred_element_type=jnp.float32)
+                attention = (summed[:, :HEAD] / summed[:, HEAD:]).astype(jnp.bfloat16)
+                outgoing[place, inner, :] = (
+                    gathered[frame, inner, :].astype(jnp.float32)
+                    + row_mods(6) * attention.astype(jnp.float32)
+                ).astype(jnp.bfloat16)
+                send_place(place, True, first, first + half)
 
     for_heads(end_rows)
 
     @pl.when(owner)
     def _():
         for place in range(frames):
-            send_place(place, False)
+            send_place(place, False, 0, span)
 
     pltpu.make_async_copy(out_ref, out_ref, out_recv).wait()
 

time: 23.6 us -> 23.9 us (1.013)
  the two profiles are of different devices: /device:TPU:11 before, /device:TPU:19 now
where the time goes in v4:
time: 23.9 us; the launch traced here: 23.7 us
  Pallas kernels  22.2 us (93%)
  local copies, waits for them, and re-layouts  0.84 us (4%)
  between operations  0.67 us (3%)
    pallas_call x1, Pallas kernels, body(): pl.pallas_call(functools.partial(kernel, devices, segments, heads, frames...  22.2 us
    reshape x1, local copies, waits for them, and re-layouts, body(): return jnp.swapaxes(tiles, 0, 1).reshape(state.shape)  0.76 us

profile of v4, /device:TPU:19, one launch (start us, length us, event | category | flops | bytes accessed | tf_op | source)
XLA Modules:
  0.0 23.7 jit_solution(14730990906208480296)
XLA Ops:
  0.7 22.2 %denoise.1 = bf16[24,32,128]{2,1,0:T(8,128)(2,1)S(1)} custom-call(s32[4]{0:T(128)} %level_ref.1, s32[4,4]{1,0:T(4,128)} %mask_ref.1, s32[1]{0:T(128)S(6)} %copy.7.offset_ref, bf16[1,32,3072]{2,1,0:T(8,128)(2,1)} %state_ref.1, f32[1,7,32,3072]{3,2,1,0:T(8,128)} %bitcast.3), custom_call_target="tpu_custom_call" | custom-call | tf_op jit(solution)/shard_map/denoise/pallas_call | solution.py:298
  22.9 0.1 copy.6
  23.0 0.8 %reshape.3 = bf16[1,32,3072]{2,1,0:T(8,128)(2,1)} reshape(bf16[32,24,128]{2,1,0:T(8,128)(2,1)S(1)} %copy.6) | data formatting | bytes 393216 | tf_op jit(solution)/shard_map/reshape | solution.py:325
